TPU v7x, 32 devices: a whole 2x2x4 slice. The times are simulated.
32 devices in a mesh: radar: 4 (over x, core), tile: 8 (over z, y).
Axes of the slice: x: 2, y: 2, z: 4, core: 2. Of those that a mesh axis runs over, the one named last changes fastest.
Arguments:
- background: float32 [3, 128, 32, 1024], P(None, 'tile', None, 'radar'), may hold values from -6 to 6
- interp: bfloat16 [2048, 128, 128], P(('radar', 'tile')), may hold values from -0.5 to 0.5
- beam: bfloat16 [2048, 3, 128], P(('radar', 'tile')), may hold values from -1 to 1
- observed: bfloat16 [2048, 128], P(('radar', 'tile')), may hold values from -6 to 6
- cell_block: int32 [2048], P(('radar', 'tile')), may hold values from 0 to 1023
- sweep_count: int32 [32, 32], P(('radar', 'tile')), may hold values from 0 to 2, as said below
Outputs:
- wind_field: float32 [3, 128, 32, 1024], P(None, 'tile', None, 'radar')
- strain: float32 [6, 128, 32, 1024], P(None, 'tile', None, 'radar')
- cost_trace: float32 [2], replicated
Inputs may be any that keep to these rules, and one draw needn't show every extreme that they name: `cell_block`: the cell block, within the owner's 16 x 32 x 256 cells of one component, read by a slot. `sweep_count`: every source device has an owning device to which all 2 of its slots are live.
All inputs are finite; a program needn't handle non-finite values.
Results may differ from a plain program's by a relative error of at most 0.0014.
Values may be sent and summed in bfloat16 or wider, within the bound.
No kernel may reach another device: no remote copies, remote signals or barrier semaphores. Data moves between devices by JAX's collectives and lax.ppermute only.
A program may use at most 64 MiB of HBM per device.

v0:
```python
import jax
import jax.numpy as jnp
from jax import lax
from jax.sharding import PartitionSpec as P

ITERS = 2
BACKGROUND_WEIGHT = 0.5
DIVERGENCE_WEIGHT = 1.0
STEP_LENGTH = 0.3
EPSILON = 1e-06


def with_halo(x, sides, width):
    for axis, dim in sides:
        size, length = (lax.axis_size(axis), x.shape[dim])
        up = [(i, (i + 1) % size) for i in range(size - 1)]
        down = [(j, i) for i, j in up]
        last = lax.slice_in_dim(x, length - width, length, axis=dim)
        first = lax.slice_in_dim(x, 0, width, axis=dim)
        before = lax.ppermute(last, axis, up)
        after = lax.ppermute(first, axis, down)
        x = jnp.concatenate([before, x, after], axis=dim)
    return x


def vertical_diff(values):
    padded = jnp.pad(values, ((0, 0), (1, 1), (0, 0)))
    return 0.5 * (padded[:, 2:, :] - padded[:, :-2, :])


def along_x(values):
    return 0.5 * (values[2:, :, 1:-1] - values[:-2, :, 1:-1])


def along_y(values):
    return 0.5 * (values[1:-1, :, 2:] - values[1:-1, :, :-2])


def along_z(values):
    return vertical_diff(values[1:-1, :, 1:-1])


def observe(cell_rows, weights, beam_rows, looked, alive_mask):
    projected = jnp.einsum("knc,ngc->nkg", cell_rows, weights, preferred_element_type=jnp.float32)
    beam_values = beam_rows.astype(jnp.float32)
    radial = jnp.sum(beam_values * projected, axis=1)
    misfit = alive_mask[:, None] * (radial - looked.astype(jnp.float32))
    adjoint = (beam_values * misfit[:, None, :]).astype(jnp.bfloat16)
    returned = jnp.einsum("nkg,ngc->knc", adjoint, weights, preferred_element_type=jnp.float32)
    return (0.5 * jnp.sum(misfit * misfit), returned)


def spread_cycle(wind_field, tile_count, radar_count):
    width_x = wind_field.shape[1]
    width_y = wind_field.shape[3]
    rim = with_halo(wind_field, (("radar", 3), ("tile", 1)), 2)
    cycle = along_x(rim[0]) + along_y(rim[1]) + along_z(rim[2])
    row_place = lax.axis_index("tile") * width_x - 1 + jnp.arange(width_x + 2, dtype=jnp.int32)
    col_place = lax.axis_index("radar") * width_y - 1 + jnp.arange(width_y + 2, dtype=jnp.int32)
    row_inside = (row_place >= 0) & (row_place < width_x * tile_count)
    col_inside = (col_place >= 0) & (col_place < width_y * radar_count)
    inside = row_inside[:, None, None] & col_inside[None, None, :]
    cycle = jnp.where(inside, cycle, 0.0)
    spread = cycle[1:-1, :, 1:-1]
    push = jnp.stack([-along_x(cycle), -along_y(cycle), -vertical_diff(spread)])
    return (spread, push)


def shards(background, interp, beam, observed, cell_block, sweep_count):
    radar_count = lax.axis_size("radar")
    tile_count = lax.axis_size("tile")
    devices = radar_count * tile_count
    width_x = background.shape[1]
    levels = background.shape[2]
    width_y = background.shape[3]
    slots = interp.shape[0] // devices
    gate_size = interp.shape[1]
    block_total = width_x * levels * width_y // gate_size
    total_cells = 3 * width_x * levels * width_y * devices
    total_gates = interp.shape[0] * devices * gate_size
    own_index = cell_block.reshape(devices, slots)
    own_alive = (
        jnp.arange(slots, dtype=jnp.int32)[None, :] < sweep_count.reshape(devices)[:, None]
    ).astype(jnp.int32)
    packed = jnp.stack([own_index, own_alive], 1)
    asked = lax.all_to_all(packed, ("radar", "tile"), split_axis=0, concat_axis=0, tiled=True)
    asked_index = asked[:, 0, :].reshape(-1)
    asked_alive = asked[:, 1, :].reshape(-1).astype(jnp.float32)
    got_weights, got_beam, got_looked = (
        lax.all_to_all(
            interp.reshape(devices, slots, gate_size, gate_size),
            ("radar", "tile"),
            split_axis=0,
            concat_axis=0,
            tiled=True,
        ),
        lax.all_to_all(
            beam.reshape(devices, slots, 3, gate_size),
            ("radar", "tile"),
            split_axis=0,
            concat_axis=0,
            tiled=True,
        ),
        lax.all_to_all(
            observed.reshape(devices, slots, gate_size),
            ("radar", "tile"),
            split_axis=0,
            concat_axis=0,
            tiled=True,
        ),
    )
    got_weights = got_weights.reshape(devices * slots, gate_size, gate_size)
    got_beam = got_beam.reshape(devices * slots, 3, gate_size)
    got_looked = got_looked.reshape(devices * slots, gate_size)
    wind_field = background
    trace = []
    for step_index in range(ITERS):
        flat = wind_field.reshape(3, block_total, gate_size)
        empty = jnp.zeros((3, block_total, gate_size), jnp.float32)
        chosen = flat[:, asked_index, :].astype(jnp.bfloat16)
        obs_cost, returned = observe(chosen, got_weights, got_beam, got_looked, asked_alive)
        obs_cost, obs_flat = (obs_cost, empty.at[:, asked_index, :].add(returned))
        obs_grad = obs_flat.reshape(wind_field.shape)
        spread, push = spread_cycle(wind_field, tile_count, radar_count)
        offset = wind_field - background
        gradient = obs_grad + BACKGROUND_WEIGHT * offset + DIVERGENCE_WEIGHT * push
        local_cost = (
            obs_cost
            + 0.5 * BACKGROUND_WEIGHT * jnp.sum(offset * offset)
            + 0.5 * DIVERGENCE_WEIGHT * jnp.sum(spread * spread)
        )
        cost_sum, square_sum = lax.psum(
            (local_cost, jnp.sum(gradient * gradient)), ("radar", "tile")
        )
        scale = jnp.sqrt(square_sum / total_cells + EPSILON)
        wind_field = wind_field - STEP_LENGTH * gradient / scale
        trace.append(cost_sum / total_gates)
    faces = with_halo(wind_field, (("radar", 3), ("tile", 1)), 1)
    east_wind, north_wind, upward_wind = (faces[0], faces[1], faces[2])
    strain = jnp.stack(
        [
            along_x(east_wind),
            along_y(north_wind),
            along_z(upward_wind),
            0.5 * (along_y(east_wind) + along_x(north_wind)),
            0.5 * (along_z(east_wind) + along_x(upward_wind)),
            0.5 * (along_z(north_wind) + along_y(upward_wind)),
        ]
    )
    return (wind_field, strain, jnp.stack(trace))


def solution(mesh):
    placed = (
        P(None, "tile", None, "radar"),
        P(("radar", "tile"), None, None),
        P(("radar", "tile"), None, None),
        P(("radar", "tile"), None),
        P(("radar", "tile")),
        P(("radar", "tile"), None),
    )
    return jax.shard_map(
        shards,
        mesh=mesh,
        in_specs=placed,
        out_specs=(P(None, "tile", None, "radar"), P(None, "tile", None, "radar"), P()),
        check_vma=False,
    )
```

profile of v0, /device:TPU:1, one launch (start us, length us, event | category | flops | bytes accessed | tf_op | source)
XLA Modules:
  0.0 292.6 jit_solution(12038039125268304084)
XLA Ops:
  2.8 7.1 %all-to-all-start = ((s32[32,2,2]{2,1,0:T(2,128)}), s32[32,2,2]{2,1,0:T(2,128)S(1)}, u32[]{:S(2)}, u32[]{:S(2)}) async-start(s32[32,2,2]{2,1,0:T(2,128)} %copy.109), calls=%async_computation | async-start | bytes 65536 | tf_op jit(solution)/shard_map/all_to_all | solution.py:86
  10.7 6.2 %all-to-all-done = s32[32,2,2]{2,1,0:T(2,128)S(1)} async-done(((s32[32,2,2]{2,1,0:T(2,128)}), s32[32,2,2]{2,1,0:T(2,128)S(1)}, u32[]{:S(2)}, u32[]{:S(2)}) %all-to-all-start) | async-done | bytes 544 | tf_op jit(solution)/shard_map/all_to_all | solution.py:86
  16.9 8.9 %all_to_all.20 = bf16[32,2,3,128]{3,1,2,0:T(2,128)(2,1)S(1)} all-to-all(bf16[32,2,3,128]{3,1,2,0:T(2,128)(2,1)S(1)} %copy.110), channel_id=1, replica_groups=mesh['radar'=4,'tile'=8] {'radar','tile'}, dimensions={0} | all-to-all | bytes 98304 | tf_op jit(solution)/shard_map/all_to_all | solution.py:97
  25.8 3.5 %all-to-all-start.2 = ((bf16[32,2,128,128]{3,2,1,0:T(8,128)(2,1)}), bf16[32,2,128,128]{3,2,1,0:T(8,128)(2,1)}, u32[]{:S(2)}, u32[]{:S(2)}) async-start(bf16[32,2,128,128]{3,2,1,0:T(8,128)(2,1)} %bitcast.87), calls=%async_computation.2 | async-start | bytes 4194304 | tf_op jit(solution)/shard_map/all_to_all | solution.py:90
  30.7 3.5 %collective-permute-start = (f32[3,16,32,2]{2,1,3,0:T(8,128)}, f32[3,16,32,2]{2,1,3,0:T(8,128)}, u32[]{:S(2)}, u32[]{:S(2)}) collective-permute-start(f32[3,16,32,2]{2,1,3,0:T(8,128)} %copy.136), channel_id=1, source_target_pairs={{0,8},{8,16},{16,24},{1,9},{9,17},{17,25},{2,10},{10,18},{18,26},{... | collective-permute-start | bytes 36872 | tf_op jit(solution)/shard_map/ppermute | solution.py:20
  35.2 1.9 collective-permute-start.1
  44.6 3.4 %collective-permute-start.2 = (f32[3,2,32,260]{3,2,1,0:T(8,128)S(1)}, f32[3,2,32,260]{3,2,1,0:T(8,128)S(1)}, u32[]{:S(2)}, u32[]{:S(2)}) collective-permute-start(f32[3,2,32,260]{3,2,1,0:T(8,128)S(1)} %get-tuple-element.19), channel_id=1, source_target_pairs={{0,1},{1,2},{2,3},{3,4},{4,5},{5,6},{6,7},{8,9},{9,10},{10,11},{11... | collective-permute-start | bytes 599048 | tf_op jit(solution)/shard_map/ppermute | solution.py:20
  49.4 10.3 %collective-permute-done.2 = f32[3,2,32,260]{3,2,1,0:T(8,128)S(1)} collective-permute-done((f32[3,2,32,260]{3,2,1,0:T(8,128)S(1)}, f32[3,2,32,260]{3,2,1,0:T(8,128)S(1)}, u32[]{:S(2)}, u32[]{:S(2)}) %collective-permute-start.2) | collective-permute-done | bytes 199712 | tf_op jit(solution)/shard_map/ppermute | solution.py:20
  59.8 1.5 collective-permute-done.3
  63.4 2.2 multiply_reduce_fusion.5
  66.5 12.5 %all-to-all-done.2 = bf16[32,2,128,128]{3,2,1,0:T(8,128)(2,1)} async-done(((bf16[32,2,128,128]{3,2,1,0:T(8,128)(2,1)}), bf16[32,2,128,128]{3,2,1,0:T(8,128)(2,1)}, u32[]{:S(2)}, u32[]{:S(2)}) %all-to-all-start.2) | async-done | bytes 2097184 | tf_op jit(solution)/shard_map/all_to_all | solution.py:90
  79.0 13.4 %all-to-all-start.3 = ((bf16[32,2,128]{2,1,0:T(2,128)(2,1)}), bf16[32,2,128]{2,1,0:T(2,128)(2,1)S(1)}, u32[]{:S(2)}, u32[]{:S(2)}) async-start(bf16[32,2,128]{2,1,0:T(2,128)(2,1)} %bitcast.7), calls=%async_computation.3 | async-start | bytes 32768 | tf_op jit(solution)/shard_map/all_to_all | solution.py:104
  92.4 2.8 fusion
  95.2 3.9 %all-to-all-done.3 = bf16[32,2,128]{2,1,0:T(2,128)(2,1)S(1)} async-done(((bf16[32,2,128]{2,1,0:T(2,128)(2,1)}), bf16[32,2,128]{2,1,0:T(2,128)(2,1)S(1)}, u32[]{:S(2)}, u32[]{:S(2)}) %all-to-all-start.3) | async-done | bytes 16416 | tf_op jit(solution)/shard_map/all_to_all | solution.py:104
  99.2 2.2 fusion.60
  101.4 1.6 broadcast.143.clone
  103.0 7.1 %scatter_fusion = f32[3,1024,128]{2,0,1:T(4,128)} fusion(f32[3,1024,128]{2,0,1:T(4,128)} %broadcast.143.clone, s32[64]{0:T(128)S(1)} %copy-done.6, f32[64,3,128]{2,1,0:T(4,128)S(1)} %fusion.60), kind=kCustom, calls=%fused_computation.2 | custom fusion | flops 24576 | bytes 295168 | tf_op jit(solution)/shard_map/scatter-add | solution.py:122
  110.1 2.8 copy.116
  113.0 1.7 reshape.212
  114.7 2.9 %multiply_reduce_fusion.3 = f32[]{:T(128)} fusion(f32[1,16,32,256]{3,2,1,0:T(8,128)} %fusion.15, f32[1,16,32,256]{3,2,1,0:T(8,128)} %get-tuple-element.39, f32[1,16,32,256]{3,2,1,0:T(8,128)} %get-tuple-element.38, f32[3,16,32,256]{3,2,1,0:T(8,128)S(1)} %reshape.212, f32[3,16,32,256]{3,2,1,0:T(8,128)S(1)} %copy-done), kind=kLoop, calls=%fused_computation.14 | loop fusion | flops 3145727 | bytes 4718596 | tf_op jit(solution)/shard_map/reduce_sum | solution.py:133
  118.3 38.0 %psum.28 = f32[]{:T(128)} all-reduce(f32[]{:T(128)} %multiply_reduce_fusion.3), channel_id=1, replica_groups=mesh['radar'=4,'tile'=8] {'radar','tile'}, use_global_device_ids=true, to_apply=%region_3.4 | all-reduce | flops 1 | bytes 8 | tf_op jit(solution)/shard_map/psum | solution.py:132
  157.0 3.2 %multiply_reduce_fusion.1 = (f32[]{:T(128)}, f32[]{:T(128)}, f32[3,16,32,256]{3,2,1,0:T(8,128)S(1)}) fusion(f32[3,16,32,256]{3,2,1,0:T(8,128)S(1)} %copy-done, f32[]{:T(128)S(6)} %sqrt.6, f32[1,16,32,256]{3,2,1,0:T(8,128)} %fusion.15, f32[1,16,32,256]{3,2,1,0:T(8,128)} %get-tuple-element.39, f32[1,16,32,256]{3,2,1,0:T(8,128)} %get-tuple-element.38, ...), kind=kLoop, calls=%fused_computation.10 | loop fusion | flops 5505022 | bytes 6291468 | tf_op jit(solution)/shard_map/reduce_sum | solution.py:129
  162.7 1.6 copy.121
  164.3 1.9 gather_fusion.1
  166.2 2.8 fusion.1
  170.5 5.1 %collective-permute-start.4 = (f32[3,16,32,2]{2,1,3,0:T(8,128)S(1)}, f32[3,16,32,2]{2,1,3,0:T(8,128)S(1)}, u32[]{:S(2)}, u32[]{:S(2)}) collective-permute-start(f32[3,16,32,2]{2,1,3,0:T(8,128)S(1)} %copy.125), channel_id=1, source_target_pairs={{0,8},{8,16},{16,24},{1,9},{9,17},{17,25},{2,10},{10,18},{18,26},{... | collective-permute-start | bytes 36872 | tf_op jit(solution)/shard_map/ppermute | solution.py:20
  175.6 2.1 copy.126
  177.7 1.9 collective-permute-start.5
  184.2 2.1 copy.128
  186.3 2.1 pad_maximum_fusion.5
  188.4 3.2 %collective-permute-start.6 = (f32[3,2,32,260]{3,2,1,0:T(8,128)}, f32[3,2,32,260]{3,2,1,0:T(8,128)}, u32[]{:S(2)}, u32[]{:S(2)}) collective-permute-start(f32[3,2,32,260]{3,2,1,0:T(8,128)} %get-tuple-element.17), channel_id=1, source_target_pairs={{0,1},{1,2},{2,3},{3,4},{4,5},{5,6},{6,7},{8,9},{9,10},{10,11},{11... | collective-permute-start | bytes 599048 | tf_op jit(solution)/shard_map/ppermute | solution.py:20
  193.0 2.2 fusion.58
  195.3 1.6 broadcast.143
  196.9 7.1 %scatter_fusion.1 = f32[3,1024,128]{2,0,1:T(4,128)} fusion(f32[3,1024,128]{2,0,1:T(4,128)} %broadcast.143, s32[64]{0:T(128)S(1)} %copy-done.7, f32[64,3,128]{2,1,0:T(4,128)S(1)} %fusion.58), kind=kCustom, calls=%fused_computation.3 | custom fusion | flops 24576 | bytes 295168 | tf_op jit(solution)/shard_map/scatter-add | solution.py:122
  204.0 2.8 copy.124
  206.8 2.7 reshape.214
  209.5 2.4 pad_maximum_fusion.1
  213.2 2.3 multiply_reduce_fusion.4
  216.2 2.1 fusion.19
  218.3 4.2 %multiply_reduce_fusion.2 = (f32[]{:T(128)}, f32[3,16,32,256]{3,2,1,0:T(8,128)}) fusion(f32[1,16,32,256]{3,2,1,0:T(8,128)} %fusion.19, f32[1,16,32,256]{3,2,1,0:T(8,128)} %get-tuple-element.43, f32[1,16,32,256]{3,2,1,0:T(8,128)} %get-tuple-element.42, f32[3,16,32,256]{3,2,1,0:T(8,128)} %reshape.214, f32[3,16,32,256]{3,2,1,0:T(8,128)S(1)} %get-tuple-element.10, ...), kind=kLoop, calls=%fused_computation.12 | loop fusion | flops 3145727 | bytes 7864324 | tf_op jit(solution)/shard_map/reduce_sum | solution.py:133
  222.5 40.7 %all-reduce.7 = (f32[]{:T(128)}, f32[]{:T(128)}, f32[]{:T(128)}) all-reduce(f32[]{:T(128)} %get-tuple-element.11, f32[]{:T(128)S(6)} %add.135, f32[]{:T(128)S(6)} %add.133), channel_id=1, replica_groups=mesh['radar'=4,'tile'=8] {'radar','tile'}, use_global_device_ids=true, to_apply=%region_7.8 | all-reduce | flops 3 | bytes 24 | tf_op jit(solution)/shard_map/psum | solution.py:132
  263.9 1.7 divide_subtract_fusion
  266.3 4.9 %collective-permute-start.8 = (f32[3,16,32,1]{2,1,3,0:T(8,128)S(1)}, f32[3,16,32,1]{2,1,3,0:T(8,128)S(1)}, u32[]{:S(2)}, u32[]{:S(2)}) collective-permute-start(f32[3,16,32,1]{2,1,3,0:T(8,128)S(1)} %copy.129), channel_id=1, source_target_pairs={{0,8},{8,16},{16,24},{1,9},{9,17},{17,25},{2,10},{10,18},{18,26},{... | collective-permute-start | bytes 18440 | tf_op jit(solution)/shard_map/ppermute | solution.py:20
  271.6 1.9 collective-permute-start.9
  275.2 1.5 collective-permute-done.9
  277.3 4.1 %collective-permute-start.10 = (f32[3,1,32,258]{3,2,1,0:T(8,128)S(1)}, f32[3,1,32,258]{3,2,1,0:T(8,128)S(1)}, u32[]{:S(2)}, u32[]{:S(2)}) collective-permute-start(f32[3,1,32,258]{3,2,1,0:T(8,128)S(1)} %get-tuple-element.15), channel_id=1, source_target_pairs={{0,1},{1,2},{2,3},{3,4},{4,5},{5,6},{6,7},{8,9},{9,10},{10,11},{11... | collective-permute-start | bytes 297224 | tf_op jit(solution)/shard_map/ppermute | solution.py:20
  283.3 4.3 %collective-permute-done.11 = f32[3,1,32,258]{3,2,1,0:T(8,128)S(1)} collective-permute-done((f32[3,1,32,258]{3,2,1,0:T(8,128)S(1)}, f32[3,1,32,258]{3,2,1,0:T(8,128)S(1)}, u32[]{:S(2)}, u32[]{:S(2)}) %collective-permute-start.11) | collective-permute-done | bytes 99104 | tf_op jit(solution)/shard_map/ppermute | solution.py:21
  291.0 1.7 copy-done.4
  (90 shorter events, 33.0 us)
Async XLA Ops:
  2.8 14.1 %all-to-all-start = ((s32[32,2,2]{2,1,0:T(2,128)}), s32[32,2,2]{2,1,0:T(2,128)S(1)}, u32[]{:S(2)}, u32[]{:S(2)}) async-start(s32[32,2,2]{2,1,0:T(2,128)} %copy.109), calls=%async_computation | async-start | bytes 65536 | tf_op jit(solution)/shard_map/all_to_all | solution.py:86
  25.8 3.5 %copy-start = (f32[3,16,32,256]{3,2,1,0:T(8,128)S(1)}, f32[3,16,32,256]{3,2,1,0:T(8,128)}, u32[]{:S(2)}) copy-start(f32[3,16,32,256]{3,2,1,0:T(8,128)} %param.6) | copy-start | bytes 4718596
  25.8 53.2 %all-to-all-start.2 = ((bf16[32,2,128,128]{3,2,1,0:T(8,128)(2,1)}), bf16[32,2,128,128]{3,2,1,0:T(8,128)(2,1)}, u32[]{:S(2)}, u32[]{:S(2)}) async-start(bf16[32,2,128,128]{3,2,1,0:T(8,128)(2,1)} %bitcast.87), calls=%async_computation.2 | async-start | bytes 4194304 | tf_op jit(solution)/shard_map/all_to_all | solution.py:90
  30.7 10.5 %collective-permute-start = (f32[3,16,32,2]{2,1,3,0:T(8,128)}, f32[3,16,32,2]{2,1,3,0:T(8,128)}, u32[]{:S(2)}, u32[]{:S(2)}) collective-permute-start(f32[3,16,32,2]{2,1,3,0:T(8,128)} %copy.136), channel_id=1, source_target_pairs={{0,8},{8,16},{16,24},{1,9},{9,17},{17,25},{2,10},{10,18},{18,26},{... | collective-permute-start | bytes 36872 | tf_op jit(solution)/shard_map/ppermute | solution.py:20
  35.2 8.0 %collective-permute-start.1 = (f32[3,16,32,2]{2,1,3,0:T(8,128)}, f32[3,16,32,2]{2,1,3,0:T(8,128)}, u32[]{:S(2)}, u32[]{:S(2)}) collective-permute-start(f32[3,16,32,2]{2,1,3,0:T(8,128)} %copy.137), channel_id=1, source_target_pairs={{8,0},{16,8},{24,16},{9,1},{17,9},{25,17},{10,2},{18,10},{26,18},{... | collective-permute-start | bytes 36872 | tf_op jit(solution)/shard_map/ppermute | solution.py:21
  38.4 0.6 copy-start.5
  44.6 15.1 %collective-permute-start.2 = (f32[3,2,32,260]{3,2,1,0:T(8,128)S(1)}, f32[3,2,32,260]{3,2,1,0:T(8,128)S(1)}, u32[]{:S(2)}, u32[]{:S(2)}) collective-permute-start(f32[3,2,32,260]{3,2,1,0:T(8,128)S(1)} %get-tuple-element.19), channel_id=1, source_target_pairs={{0,1},{1,2},{2,3},{3,4},{4,5},{5,6},{6,7},{8,9},{9,10},{10,11},{11... | collective-permute-start | bytes 599048 | tf_op jit(solution)/shard_map/ppermute | solution.py:20
  48.0 13.2 %collective-permute-start.3 = (f32[3,2,32,260]{3,2,1,0:T(8,128)S(1)}, f32[3,2,32,260]{3,2,1,0:T(8,128)S(1)}, u32[]{:S(2)}, u32[]{:S(2)}) collective-permute-start(f32[3,2,32,260]{3,2,1,0:T(8,128)S(1)} %get-tuple-element.20), channel_id=1, source_target_pairs={{1,0},{2,1},{3,2},{4,3},{5,4},{6,5},{7,6},{9,8},{10,9},{11,10},{12... | collective-permute-start | bytes 599048 | tf_op jit(solution)/shard_map/ppermute | solution.py:21
  65.6 33.5 %copy-start.8 = (f32[64]{0:T(128)S(1)}, f32[64]{0:T(128)}, u32[]{:S(2)}) copy-start(f32[64]{0:T(128)} %convert_element_type.74) | copy-start | bytes 772
  79.0 20.1 %all-to-all-start.3 = ((bf16[32,2,128]{2,1,0:T(2,128)(2,1)}), bf16[32,2,128]{2,1,0:T(2,128)(2,1)S(1)}, u32[]{:S(2)}, u32[]{:S(2)}) async-start(bf16[32,2,128]{2,1,0:T(2,128)(2,1)} %bitcast.7), calls=%async_computation.3 | async-start | bytes 32768 | tf_op jit(solution)/shard_map/all_to_all | solution.py:104
  99.2 3.8 %copy-start.6 = (s32[64]{0:T(128)S(1)}, s32[64]{0:T(128)}, u32[]{:S(2)}) copy-start(s32[64]{0:T(128)} %copy-done.5) | copy-start | bytes 772
  114.7 3.0 %copy-start.2 = (f32[3,16,32,256]{3,2,1,0:T(8,128)}, f32[3,16,32,256]{3,2,1,0:T(8,128)S(1)}, u32[]{:S(2)}) copy-start(f32[3,16,32,256]{3,2,1,0:T(8,128)S(1)} %reshape.212) | copy-start | bytes 4718596
  161.3 1.4 copy-start.3
  166.2 13.4 %copy-start.9 = (f32[64]{0:T(128)S(1)}, f32[64]{0:T(128)}, u32[]{:S(2)}) copy-start(f32[64]{0:T(128)} %convert_element_type.74) | copy-start | bytes 772
  170.5 12.5 %collective-permute-start.4 = (f32[3,16,32,2]{2,1,3,0:T(8,128)S(1)}, f32[3,16,32,2]{2,1,3,0:T(8,128)S(1)}, u32[]{:S(2)}, u32[]{:S(2)}) collective-permute-start(f32[3,16,32,2]{2,1,3,0:T(8,128)S(1)} %copy.125), channel_id=1, source_target_pairs={{0,8},{8,16},{16,24},{1,9},{9,17},{17,25},{2,10},{10,18},{18,26},{... | collective-permute-start | bytes 36872 | tf_op jit(solution)/shard_map/ppermute | solution.py:20
  177.7 6.5 %collective-permute-start.5 = (f32[3,16,32,2]{2,1,3,0:T(8,128)}, f32[3,16,32,2]{2,1,3,0:T(8,128)}, u32[]{:S(2)}, u32[]{:S(2)}) collective-permute-start(f32[3,16,32,2]{2,1,3,0:T(8,128)} %copy.126), channel_id=1, source_target_pairs={{8,0},{16,8},{24,16},{9,1},{17,9},{25,17},{10,2},{18,10},{26,18},{... | collective-permute-start | bytes 36872 | tf_op jit(solution)/shard_map/ppermute | solution.py:21
  188.4 21.1 %collective-permute-start.6 = (f32[3,2,32,260]{3,2,1,0:T(8,128)}, f32[3,2,32,260]{3,2,1,0:T(8,128)}, u32[]{:S(2)}, u32[]{:S(2)}) collective-permute-start(f32[3,2,32,260]{3,2,1,0:T(8,128)} %get-tuple-element.17), channel_id=1, source_target_pairs={{0,1},{1,2},{2,3},{3,4},{4,5},{5,6},{6,7},{8,9},{9,10},{10,11},{11... | collective-permute-start | bytes 599048 | tf_op jit(solution)/shard_map/ppermute | solution.py:20
  191.6 5.3 %copy-start.7 = (s32[64]{0:T(128)S(1)}, s32[64]{0:T(128)}, u32[]{:S(2)}) copy-start(s32[64]{0:T(128)} %copy-done.5) | copy-start | bytes 772
  191.6 17.9 %collective-permute-start.7 = (f32[3,2,32,260]{3,2,1,0:T(8,128)}, f32[3,2,32,260]{3,2,1,0:T(8,128)}, u32[]{:S(2)}, u32[]{:S(2)}) collective-permute-start(f32[3,2,32,260]{3,2,1,0:T(8,128)} %get-tuple-element.18), channel_id=1, source_target_pairs={{1,0},{2,1},{3,2},{4,3},{5,4},{6,5},{7,6},{9,8},{10,9},{11,10},{12... | collective-permute-start | bytes 599048 | tf_op jit(solution)/shard_map/ppermute | solution.py:21
  265.6 21.9 %copy-start.1 = (f32[3,16,32,256]{3,2,1,0:T(8,128)}, f32[3,16,32,256]{3,2,1,0:T(8,128)S(1)}, u32[]{:S(2)}) copy-start(f32[3,16,32,256]{3,2,1,0:T(8,128)S(1)} %divide_subtract_fusion) | copy-start | bytes 4718596
  266.3 8.5 %collective-permute-start.8 = (f32[3,16,32,1]{2,1,3,0:T(8,128)S(1)}, f32[3,16,32,1]{2,1,3,0:T(8,128)S(1)}, u32[]{:S(2)}, u32[]{:S(2)}) collective-permute-start(f32[3,16,32,1]{2,1,3,0:T(8,128)S(1)} %copy.129), channel_id=1, source_target_pairs={{0,8},{8,16},{16,24},{1,9},{9,17},{17,25},{2,10},{10,18},{18,26},{... | collective-permute-start | bytes 18440 | tf_op jit(solution)/shard_map/ppermute | solution.py:20
  271.6 5.1 %collective-permute-start.9 = (f32[3,16,32,1]{2,1,3,0:T(8,128)S(1)}, f32[3,16,32,1]{2,1,3,0:T(8,128)S(1)}, u32[]{:S(2)}, u32[]{:S(2)}) collective-permute-start(f32[3,16,32,1]{2,1,3,0:T(8,128)S(1)} %copy.130), channel_id=1, source_target_pairs={{8,0},{16,8},{24,16},{9,1},{17,9},{25,17},{10,2},{18,10},{26,18},{... | collective-permute-start | bytes 18440 | tf_op jit(solution)/shard_map/ppermute | solution.py:21
  277.3 6.0 %collective-permute-start.10 = (f32[3,1,32,258]{3,2,1,0:T(8,128)S(1)}, f32[3,1,32,258]{3,2,1,0:T(8,128)S(1)}, u32[]{:S(2)}, u32[]{:S(2)}) collective-permute-start(f32[3,1,32,258]{3,2,1,0:T(8,128)S(1)} %get-tuple-element.15), channel_id=1, source_target_pairs={{0,1},{1,2},{2,3},{3,4},{4,5},{5,6},{6,7},{8,9},{9,10},{10,11},{11... | collective-permute-start | bytes 297224 | tf_op jit(solution)/shard_map/ppermute | solution.py:20
  281.4 6.2 %collective-permute-start.11 = (f32[3,1,32,258]{3,2,1,0:T(8,128)S(1)}, f32[3,1,32,258]{3,2,1,0:T(8,128)S(1)}, u32[]{:S(2)}, u32[]{:S(2)}) collective-permute-start(f32[3,1,32,258]{3,2,1,0:T(8,128)S(1)} %get-tuple-element.16), channel_id=1, source_target_pairs={{1,0},{2,1},{3,2},{4,3},{5,4},{6,5},{7,6},{9,8},{10,9},{11,10},{12... | collective-permute-start | bytes 297224 | tf_op jit(solution)/shard_map/ppermute | solution.py:21
  290.9 1.7 copy-start.4
where the time goes:
time: 294 us; the launch traced here: 293 us
  blocking collectives  87.6 us (30%)
  starting transfers between devices  58 us (20%)
  other arithmetic  46.2 us (16%)
  waiting for transfers between devices  42 us (14%)
  local copies, waits for them, and re-layouts  41 us (14%)
  matrix products  10 us (3%)
  between operations  7.66 us (3%)
    psum x2, blocking collectives, shards(): lax.psum((local_cost, jnp.sum(gradient * gradient)), ('radar', 'tile'))  78.7 us
    ppermute x6, starting transfers between devices, with_halo(): before = lax.ppermute(last, axis, up)  24.3 us
    scatter-add x2, other arithmetic, shards(): obs_cost, obs_flat = (obs_cost, empty.at[:, asked_index, :].add(returned))  14.2 us
    all_to_all x1, starting transfers between devices, shards(): lax.all_to_all(observed.reshape(devices, slots, gate_size), ('radar', 'ti...  13.4 us
    all_to_all x1, waiting for transfers between devices, shards(): lax.all_to_all(interp.reshape(devices, slots, gate_size, gate_size), ('ra...  12.5 us
    ppermute x6, waiting for transfers between devices, with_halo(): before = lax.ppermute(last, axis, up)  11.2 us
    ppermute x6, starting transfers between devices, with_halo(): after = lax.ppermute(first, axis, down)  9.74 us
    all_to_all x1, blocking collectives, shards(): lax.all_to_all(beam.reshape(devices, slots, 3, gate_size), ('radar', 'til...  8.91 us
  transfers between devices with their start and end apart: 15, of which 9 were waited for; matrix products, arithmetic and copies ran while one was open for 13% of the time, Pallas kernels for 0%

commit v1 on v0

--- a/solution.py
+++ b/solution.py
@@ -2,6 +2,7 @@
 import jax.numpy as jnp
 from jax import lax
 from jax.sharding import PartitionSpec as P
+from jax.lax import psum
 
 ITERS = 2
 BACKGROUND_WEIGHT = 0.5
@@ -129,8 +130,11 @@
             + 0.5 * BACKGROUND_WEIGHT * jnp.sum(offset * offset)
             + 0.5 * DIVERGENCE_WEIGHT * jnp.sum(spread * spread)
         )
-        cost_sum, square_sum = lax.psum(
-            (local_cost, jnp.sum(gradient * gradient)), ("radar", "tile")
+        prepare_zone_all = lambda in_array, peer_axis, along_axis: psum(
+            psum(in_array, peer_axis), along_axis
+        )
+        cost_sum, square_sum = prepare_zone_all(
+            (local_cost, jnp.sum(gradient * gradient)), "tile", "radar"
         )
         scale = jnp.sqrt(square_sum / total_cells + EPSILON)
         wind_field = wind_field - STEP_LENGTH * gradient / scale

time: 294 us -> 261 us (0.89)
  blocking collectives: 87.6 us -> 60.7 us
  starting transfers between devices: 58 us -> 52.6 us
    psum x2 -> x4, blocking collectives: 78.7 us -> 51.8 us  [the longest x2 31 us: shards(): psum(in_array, peer_axis)]
    ppermute x6, starting transfers between devices: 24.3 us -> 18.6 us  [with_halo(): before = lax.ppermute(last, axis, up)]
  transfers between devices with their start and end apart: 15 -> 15, of which waited for: 9 -> 9; matrix products, arithmetic and copies ran while one was open for 13% -> 15% of each run, Pallas kernels for 0% -> 0%
where the time goes in v1:
time: 261 us; the launch traced here: 260 us
  blocking collectives  60.7 us (23%)
  starting transfers between devices  52.6 us (20%)
  other arithmetic  46.2 us (18%)
  waiting for transfers between devices  41.5 us (16%)
  local copies, waits for them, and re-layouts  41 us (16%)
  matrix products  10 us (4%)
  between operations  7.66 us (3%)
    psum x2, blocking collectives, shards(): psum(in_array, peer_axis)  31 us
    psum x2, blocking collectives, shards(): psum(psum(in_array, peer_axis), along_axis)  20.7 us
    ppermute x6, starting transfers between devices, with_halo(): before = lax.ppermute(last, axis, up)  18.6 us
    scatter-add x2, other arithmetic, shards(): obs_cost, obs_flat = (obs_cost, empty.at[:, asked_index, :].add(returned))  14.2 us
    all_to_all x1, starting transfers between devices, shards(): lax.all_to_all(observed.reshape(devices, slots, gate_size), ('radar', 'ti...  13.4 us
    all_to_all x1, waiting for transfers between devices, shards(): lax.all_to_all(interp.reshape(devices, slots, gate_size, gate_size), ('ra...  12.5 us
    ppermute x6, waiting for transfers between devices, with_halo(): before = lax.ppermute(last, axis, up)  11.2 us
    ppermute x6, starting transfers between devices, with_halo(): after = lax.ppermute(first, axis, down)  9.96 us
  transfers between devices with their start and end apart: 15, of which 9 were waited for; matrix products, arithmetic and copies ran while one was open for 15% of the time, Pallas kernels for 0%

profile of v1, /device:TPU:1, one launch (start us, length us, event | category | flops | bytes accessed | tf_op | source)
XLA Modules:
  0.0 259.8 jit_solution(8950969072427879582)
XLA Ops:
  2.8 7.1 %all-to-all-start = ((s32[32,2,2]{2,1,0:T(2,128)}), s32[32,2,2]{2,1,0:T(2,128)S(1)}, u32[]{:S(2)}, u32[]{:S(2)}) async-start(s32[32,2,2]{2,1,0:T(2,128)} %copy.109), calls=%async_computation | async-start | bytes 65536 | tf_op jit(solution)/shard_map/all_to_all | solution.py:87
  10.7 6.2 %all-to-all-done = s32[32,2,2]{2,1,0:T(2,128)S(1)} async-done(((s32[32,2,2]{2,1,0:T(2,128)}), s32[32,2,2]{2,1,0:T(2,128)S(1)}, u32[]{:S(2)}, u32[]{:S(2)}) %all-to-all-start) | async-done | bytes 544 | tf_op jit(solution)/shard_map/all_to_all | solution.py:87
  16.9 8.9 %all_to_all.20 = bf16[32,2,3,128]{3,1,2,0:T(2,128)(2,1)S(1)} all-to-all(bf16[32,2,3,128]{3,1,2,0:T(2,128)(2,1)S(1)} %copy.110), channel_id=1, replica_groups=mesh['radar'=4,'tile'=8] {'radar','tile'}, dimensions={0} | all-to-all | bytes 98304 | tf_op jit(solution)/shard_map/all_to_all | solution.py:98
  25.8 3.5 %all-to-all-start.2 = ((bf16[32,2,128,128]{3,2,1,0:T(8,128)(2,1)}), bf16[32,2,128,128]{3,2,1,0:T(8,128)(2,1)}, u32[]{:S(2)}, u32[]{:S(2)}) async-start(bf16[32,2,128,128]{3,2,1,0:T(8,128)(2,1)} %bitcast.87), calls=%async_computation.2 | async-start | bytes 4194304 | tf_op jit(solution)/shard_map/all_to_all | solution.py:91
  30.7 3.5 %collective-permute-start = (f32[3,16,32,2]{2,1,3,0:T(8,128)}, f32[3,16,32,2]{2,1,3,0:T(8,128)}, u32[]{:S(2)}, u32[]{:S(2)}) collective-permute-start(f32[3,16,32,2]{2,1,3,0:T(8,128)} %copy.136), channel_id=1, source_target_pairs={{0,8},{8,16},{16,24},{1,9},{9,17},{17,25},{2,10},{10,18},{18,26},{... | collective-permute-start | bytes 36872 | tf_op jit(solution)/shard_map/ppermute | solution.py:21
  35.2 1.9 collective-permute-start.1
  44.6 3.4 %collective-permute-start.2 = (f32[3,2,32,260]{3,2,1,0:T(8,128)S(1)}, f32[3,2,32,260]{3,2,1,0:T(8,128)S(1)}, u32[]{:S(2)}, u32[]{:S(2)}) collective-permute-start(f32[3,2,32,260]{3,2,1,0:T(8,128)S(1)} %get-tuple-element.22), channel_id=1, source_target_pairs={{0,1},{1,2},{2,3},{3,4},{4,5},{5,6},{6,7},{8,9},{9,10},{10,11},{11... | collective-permute-start | bytes 599048 | tf_op jit(solution)/shard_map/ppermute | solution.py:21
  49.4 10.3 %collective-permute-done.2 = f32[3,2,32,260]{3,2,1,0:T(8,128)S(1)} collective-permute-done((f32[3,2,32,260]{3,2,1,0:T(8,128)S(1)}, f32[3,2,32,260]{3,2,1,0:T(8,128)S(1)}, u32[]{:S(2)}, u32[]{:S(2)}) %collective-permute-start.2) | collective-permute-done | bytes 199712 | tf_op jit(solution)/shard_map/ppermute | solution.py:21
  63.4 2.2 multiply_reduce_fusion.5
  66.5 12.5 %all-to-all-done.2 = bf16[32,2,128,128]{3,2,1,0:T(8,128)(2,1)} async-done(((bf16[32,2,128,128]{3,2,1,0:T(8,128)(2,1)}), bf16[32,2,128,128]{3,2,1,0:T(8,128)(2,1)}, u32[]{:S(2)}, u32[]{:S(2)}) %all-to-all-start.2) | async-done | bytes 2097184 | tf_op jit(solution)/shard_map/all_to_all | solution.py:91
  79.0 13.4 %all-to-all-start.3 = ((bf16[32,2,128]{2,1,0:T(2,128)(2,1)}), bf16[32,2,128]{2,1,0:T(2,128)(2,1)S(1)}, u32[]{:S(2)}, u32[]{:S(2)}) async-start(bf16[32,2,128]{2,1,0:T(2,128)(2,1)} %bitcast.7), calls=%async_computation.3 | async-start | bytes 32768 | tf_op jit(solution)/shard_map/all_to_all | solution.py:105
  92.4 2.8 %fusion = f32[64,128]{1,0:T(8,128)S(1)} fusion(bf16[64,128,128]{2,1,0:T(8,128)(2,1)} %bitcast.6, f32[64,3,128]{2,0,1:T(8,128)S(1)} %bitcast.83, bf16[64,3,128]{2,1,0:T(4,128)(2,1)S(1)} %gather_fusion), kind=kOutput, calls=%fused_computation.21 | convolution fusion | flops 6332416 | bytes 2277376 | tf_op jit(solution)/shard_map/knc,ngc->nkg/dot_general | solution.py:45
  95.2 3.9 %all-to-all-done.3 = bf16[32,2,128]{2,1,0:T(2,128)(2,1)S(1)} async-done(((bf16[32,2,128]{2,1,0:T(2,128)(2,1)}), bf16[32,2,128]{2,1,0:T(2,128)(2,1)S(1)}, u32[]{:S(2)}, u32[]{:S(2)}) %all-to-all-start.3) | async-done | bytes 16416 | tf_op jit(solution)/shard_map/all_to_all | solution.py:105
  99.2 2.2 fusion.60
  101.4 1.6 broadcast.143.clone
  103.0 7.1 %scatter_fusion = f32[3,1024,128]{2,0,1:T(4,128)} fusion(f32[3,1024,128]{2,0,1:T(4,128)} %broadcast.143.clone, s32[64]{0:T(128)S(1)} %copy-done.6, f32[64,3,128]{2,1,0:T(4,128)S(1)} %fusion.60), kind=kCustom, calls=%fused_computation.2 | custom fusion | flops 24576 | bytes 295168 | tf_op jit(solution)/shard_map/scatter-add | solution.py:123
  110.1 2.8 %copy.116 = f32[3,1024,128]{2,1,0:T(8,128)} copy(f32[3,1024,128]{2,0,1:T(4,128)} %scatter_fusion) | data formatting | bytes 3145728 | tf_op jit(solution)/shard_map/scatter-add | solution.py:123
  113.0 1.7 reshape.212
  114.7 2.9 %multiply_reduce_fusion.3 = f32[]{:T(128)} fusion(f32[1,16,32,256]{3,2,1,0:T(8,128)} %fusion.15, f32[1,16,32,256]{3,2,1,0:T(8,128)} %get-tuple-element.42, f32[1,16,32,256]{3,2,1,0:T(8,128)} %get-tuple-element.41, f32[3,16,32,256]{3,2,1,0:T(8,128)S(1)} %reshape.212, f32[3,16,32,256]{3,2,1,0:T(8,128)S(1)} %copy-done), kind=kLoop, calls=%fused_computation.14 | loop fusion | flops 3145727 | bytes 4718596 | tf_op jit(solution)/shard_map/reduce_sum | solution.py:137
  117.7 14.7 %psum.56 = f32[]{:T(128)} all-reduce(f32[]{:T(128)} %multiply_reduce_fusion.3), channel_id=1, replica_groups=mesh['radar'=4,'tile'=8] {'tile'}, use_global_device_ids=true, to_apply=%region_3.4 | all-reduce | flops 1 | bytes 8 | tf_op jit(solution)/shard_map/psum | solution.py:134
  133.0 10.2 %psum.57 = f32[]{:T(128)} all-reduce(f32[]{:T(128)} %psum.56), channel_id=1, replica_groups=mesh['radar'=4,'tile'=8] {'radar'}, use_global_device_ids=true, to_apply=%region_4.5 | all-reduce | flops 1 | bytes 8 | tf_op jit(solution)/shard_map/psum | solution.py:133
  143.9 3.2 %multiply_reduce_fusion.1 = (f32[]{:T(128)}, f32[]{:T(128)}, f32[3,16,32,256]{3,2,1,0:T(8,128)S(1)}) fusion(f32[3,16,32,256]{3,2,1,0:T(8,128)S(1)} %copy-done, f32[]{:T(128)S(6)} %sqrt.6, f32[1,16,32,256]{3,2,1,0:T(8,128)} %fusion.15, f32[1,16,32,256]{3,2,1,0:T(8,128)} %get-tuple-element.42, f32[1,16,32,256]{3,2,1,0:T(8,128)} %get-tuple-element.41, ...), kind=kLoop, calls=%fused_computation.10 | loop fusion | flops 5505022 | bytes 6291468 | tf_op jit(solution)/shard_map/reduce_sum | solution.py:130
  149.6 1.6 copy.121
  151.2 1.9 gather_fusion.1
  153.1 2.8 %fusion.1 = f32[64,128]{1,0:T(8,128)S(1)} fusion(bf16[64,128,128]{2,1,0:T(8,128)(2,1)} %bitcast.6, f32[64,3,128]{2,0,1:T(8,128)S(1)} %bitcast.85, bf16[64,3,128]{2,1,0:T(4,128)(2,1)S(1)} %gather_fusion.1), kind=kOutput, calls=%fused_computation.22 | convolution fusion | flops 6332416 | bytes 2277376 | tf_op jit(solution)/shard_map/knc,ngc->nkg/dot_general | solution.py:45
  157.4 3.3 %collective-permute-start.4 = (f32[3,16,32,2]{2,1,3,0:T(8,128)S(1)}, f32[3,16,32,2]{2,1,3,0:T(8,128)S(1)}, u32[]{:S(2)}, u32[]{:S(2)}) collective-permute-start(f32[3,16,32,2]{2,1,3,0:T(8,128)S(1)} %copy.125), channel_id=1, source_target_pairs={{0,8},{8,16},{16,24},{1,9},{9,17},{17,25},{2,10},{10,18},{18,26},{... | collective-permute-start | bytes 36872 | tf_op jit(solution)/shard_map/ppermute | solution.py:21
  160.7 2.1 copy.126
  162.8 1.9 collective-permute-start.5
  169.3 2.1 copy.128
  171.4 2.1 pad_maximum_fusion.5
  173.5 3.2 %collective-permute-start.6 = (f32[3,2,32,260]{3,2,1,0:T(8,128)}, f32[3,2,32,260]{3,2,1,0:T(8,128)}, u32[]{:S(2)}, u32[]{:S(2)}) collective-permute-start(f32[3,2,32,260]{3,2,1,0:T(8,128)} %get-tuple-element.20), channel_id=1, source_target_pairs={{0,1},{1,2},{2,3},{3,4},{4,5},{5,6},{6,7},{8,9},{9,10},{10,11},{11... | collective-permute-start | bytes 599048 | tf_op jit(solution)/shard_map/ppermute | solution.py:21
  178.1 2.2 fusion.58
  180.4 1.6 broadcast.143
  182.0 7.1 %scatter_fusion.1 = f32[3,1024,128]{2,0,1:T(4,128)} fusion(f32[3,1024,128]{2,0,1:T(4,128)} %broadcast.143, s32[64]{0:T(128)S(1)} %copy-done.7, f32[64,3,128]{2,1,0:T(4,128)S(1)} %fusion.58), kind=kCustom, calls=%fused_computation.3 | custom fusion | flops 24576 | bytes 295168 | tf_op jit(solution)/shard_map/scatter-add | solution.py:123
  189.1 2.8 %copy.124 = f32[3,1024,128]{2,1,0:T(8,128)} copy(f32[3,1024,128]{2,0,1:T(4,128)} %scatter_fusion.1) | data formatting | bytes 3145728 | tf_op jit(solution)/shard_map/scatter-add | solution.py:123
  191.9 2.7 %reshape.214 = f32[3,16,32,256]{3,2,1,0:T(8,128)} reshape(f32[3,1024,128]{2,1,0:T(8,128)} %copy.124) | data formatting | bytes 3145728 | tf_op jit(solution)/shard_map/reshape | solution.py:124
  194.6 2.4 pad_maximum_fusion.1
  198.3 2.3 multiply_reduce_fusion.4
  201.3 2.1 fusion.19
  203.4 4.2 %multiply_reduce_fusion.2 = (f32[]{:T(128)}, f32[3,16,32,256]{3,2,1,0:T(8,128)}) fusion(f32[1,16,32,256]{3,2,1,0:T(8,128)} %fusion.19, f32[1,16,32,256]{3,2,1,0:T(8,128)} %get-tuple-element.46, f32[1,16,32,256]{3,2,1,0:T(8,128)} %get-tuple-element.45, f32[3,16,32,256]{3,2,1,0:T(8,128)} %reshape.214, f32[3,16,32,256]{3,2,1,0:T(8,128)S(1)} %get-tuple-element.13, ...), kind=kLoop, calls=%fused_computation.12 | loop fusion | flops 3145727 | bytes 7864324 | tf_op jit(solution)/shard_map/reduce_sum | solution.py:137
  207.6 16.4 %all-reduce.7 = (f32[]{:T(128)}, f32[]{:T(128)}, f32[]{:T(128)}) all-reduce(f32[]{:T(128)} %get-tuple-element.14, f32[]{:T(128)S(6)} %add.143, f32[]{:T(128)S(6)} %add.141), channel_id=1, replica_groups=mesh['radar'=4,'tile'=8] {'tile'}, use_global_device_ids=true, to_apply=%region_8.9 | all-reduce | flops 3 | bytes 24 | tf_op jit(solution)/shard_map/psum | solution.py:134
  223.9 10.5 %all-reduce.8 = (f32[]{:T(128)}, f32[]{:T(128)}, f32[]{:T(128)}) all-reduce(f32[]{:T(128)} %get-tuple-element.7, f32[]{:T(128)} %get-tuple-element.8, f32[]{:T(128)} %get-tuple-element.9), channel_id=1, replica_groups=mesh['radar'=4,'tile'=8] {'radar'}, use_global_device_ids=true, to_apply=%region_9.10 | all-reduce | flops 3 | bytes 24 | tf_op jit(solution)/shard_map/psum | solution.py:133
  235.2 1.7 divide_subtract_fusion
  237.6 3.9 %collective-permute-start.8 = (f32[3,16,32,1]{2,1,3,0:T(8,128)S(1)}, f32[3,16,32,1]{2,1,3,0:T(8,128)S(1)}, u32[]{:S(2)}, u32[]{:S(2)}) collective-permute-start(f32[3,16,32,1]{2,1,3,0:T(8,128)S(1)} %copy.129), channel_id=1, source_target_pairs={{0,8},{8,16},{16,24},{1,9},{9,17},{17,25},{2,10},{10,18},{18,26},{... | collective-permute-start | bytes 18440 | tf_op jit(solution)/shard_map/ppermute | solution.py:21
  241.8 1.9 collective-permute-start.9
  248.8 1.5 collective-permute-start.11
  250.9 3.8 %collective-permute-done.11 = f32[3,1,32,258]{3,2,1,0:T(8,128)S(1)} collective-permute-done((f32[3,1,32,258]{3,2,1,0:T(8,128)S(1)}, f32[3,1,32,258]{3,2,1,0:T(8,128)S(1)}, u32[]{:S(2)}, u32[]{:S(2)}) %collective-permute-start.11) | collective-permute-done | bytes 99104 | tf_op jit(solution)/shard_map/ppermute | solution.py:22
  258.1 1.7 copy-done.4
  (92 shorter events, 36.0 us)
Async XLA Ops:
  2.8 14.1 %all-to-all-start = ((s32[32,2,2]{2,1,0:T(2,128)}), s32[32,2,2]{2,1,0:T(2,128)S(1)}, u32[]{:S(2)}, u32[]{:S(2)}) async-start(s32[32,2,2]{2,1,0:T(2,128)} %copy.109), calls=%async_computation | async-start | bytes 65536 | tf_op jit(solution)/shard_map/all_to_all | solution.py:87
  25.8 3.5 %copy-start = (f32[3,16,32,256]{3,2,1,0:T(8,128)S(1)}, f32[3,16,32,256]{3,2,1,0:T(8,128)}, u32[]{:S(2)}) copy-start(f32[3,16,32,256]{3,2,1,0:T(8,128)} %param.6) | copy-start | bytes 4718596
  25.8 53.2 %all-to-all-start.2 = ((bf16[32,2,128,128]{3,2,1,0:T(8,128)(2,1)}), bf16[32,2,128,128]{3,2,1,0:T(8,128)(2,1)}, u32[]{:S(2)}, u32[]{:S(2)}) async-start(bf16[32,2,128,128]{3,2,1,0:T(8,128)(2,1)} %bitcast.87), calls=%async_computation.2 | async-start | bytes 4194304 | tf_op jit(solution)/shard_map/all_to_all | solution.py:91
  30.7 10.5 %collective-permute-start = (f32[3,16,32,2]{2,1,3,0:T(8,128)}, f32[3,16,32,2]{2,1,3,0:T(8,128)}, u32[]{:S(2)}, u32[]{:S(2)}) collective-permute-start(f32[3,16,32,2]{2,1,3,0:T(8,128)} %copy.136), channel_id=1, source_target_pairs={{0,8},{8,16},{16,24},{1,9},{9,17},{17,25},{2,10},{10,18},{18,26},{... | collective-permute-start | bytes 36872 | tf_op jit(solution)/shard_map/ppermute | solution.py:21
  35.2 8.0 %collective-permute-start.1 = (f32[3,16,32,2]{2,1,3,0:T(8,128)}, f32[3,16,32,2]{2,1,3,0:T(8,128)}, u32[]{:S(2)}, u32[]{:S(2)}) collective-permute-start(f32[3,16,32,2]{2,1,3,0:T(8,128)} %copy.137), channel_id=1, source_target_pairs={{8,0},{16,8},{24,16},{9,1},{17,9},{25,17},{10,2},{18,10},{26,18},{... | collective-permute-start | bytes 36872 | tf_op jit(solution)/shard_map/ppermute | solution.py:22
  38.4 0.6 copy-start.5
  44.6 15.1 %collective-permute-start.2 = (f32[3,2,32,260]{3,2,1,0:T(8,128)S(1)}, f32[3,2,32,260]{3,2,1,0:T(8,128)S(1)}, u32[]{:S(2)}, u32[]{:S(2)}) collective-permute-start(f32[3,2,32,260]{3,2,1,0:T(8,128)S(1)} %get-tuple-element.22), channel_id=1, source_target_pairs={{0,1},{1,2},{2,3},{3,4},{4,5},{5,6},{6,7},{8,9},{9,10},{10,11},{11... | collective-permute-start | bytes 599048 | tf_op jit(solution)/shard_map/ppermute | solution.py:21
  48.0 13.2 %collective-permute-start.3 = (f32[3,2,32,260]{3,2,1,0:T(8,128)S(1)}, f32[3,2,32,260]{3,2,1,0:T(8,128)S(1)}, u32[]{:S(2)}, u32[]{:S(2)}) collective-permute-start(f32[3,2,32,260]{3,2,1,0:T(8,128)S(1)} %get-tuple-element.23), channel_id=1, source_target_pairs={{1,0},{2,1},{3,2},{4,3},{5,4},{6,5},{7,6},{9,8},{10,9},{11,10},{12... | collective-permute-start | bytes 599048 | tf_op jit(solution)/shard_map/ppermute | solution.py:22
  65.6 33.5 %copy-start.8 = (f32[64]{0:T(128)S(1)}, f32[64]{0:T(128)}, u32[]{:S(2)}) copy-start(f32[64]{0:T(128)} %convert_element_type.74) | copy-start | bytes 772
  79.0 20.1 %all-to-all-start.3 = ((bf16[32,2,128]{2,1,0:T(2,128)(2,1)}), bf16[32,2,128]{2,1,0:T(2,128)(2,1)S(1)}, u32[]{:S(2)}, u32[]{:S(2)}) async-start(bf16[32,2,128]{2,1,0:T(2,128)(2,1)} %bitcast.7), calls=%async_computation.3 | async-start | bytes 32768 | tf_op jit(solution)/shard_map/all_to_all | solution.py:105
  99.2 3.8 %copy-start.6 = (s32[64]{0:T(128)S(1)}, s32[64]{0:T(128)}, u32[]{:S(2)}) copy-start(s32[64]{0:T(128)} %copy-done.5) | copy-start | bytes 772
  114.7 3.0 %copy-start.2 = (f32[3,16,32,256]{3,2,1,0:T(8,128)}, f32[3,16,32,256]{3,2,1,0:T(8,128)S(1)}, u32[]{:S(2)}) copy-start(f32[3,16,32,256]{3,2,1,0:T(8,128)S(1)} %reshape.212) | copy-start | bytes 4718596
  148.2 1.4 copy-start.3
  153.1 11.6 %copy-start.9 = (f32[64]{0:T(128)S(1)}, f32[64]{0:T(128)}, u32[]{:S(2)}) copy-start(f32[64]{0:T(128)} %convert_element_type.74) | copy-start | bytes 772
  157.4 10.7 %collective-permute-start.4 = (f32[3,16,32,2]{2,1,3,0:T(8,128)S(1)}, f32[3,16,32,2]{2,1,3,0:T(8,128)S(1)}, u32[]{:S(2)}, u32[]{:S(2)}) collective-permute-start(f32[3,16,32,2]{2,1,3,0:T(8,128)S(1)} %copy.125), channel_id=1, source_target_pairs={{0,8},{8,16},{16,24},{1,9},{9,17},{17,25},{2,10},{10,18},{18,26},{... | collective-permute-start | bytes 36872 | tf_op jit(solution)/shard_map/ppermute | solution.py:21
  162.8 6.5 %collective-permute-start.5 = (f32[3,16,32,2]{2,1,3,0:T(8,128)}, f32[3,16,32,2]{2,1,3,0:T(8,128)}, u32[]{:S(2)}, u32[]{:S(2)}) collective-permute-start(f32[3,16,32,2]{2,1,3,0:T(8,128)} %copy.126), channel_id=1, source_target_pairs={{8,0},{16,8},{24,16},{9,1},{17,9},{25,17},{10,2},{18,10},{26,18},{... | collective-permute-start | bytes 36872 | tf_op jit(solution)/shard_map/ppermute | solution.py:22
  173.5 21.1 %collective-permute-start.6 = (f32[3,2,32,260]{3,2,1,0:T(8,128)}, f32[3,2,32,260]{3,2,1,0:T(8,128)}, u32[]{:S(2)}, u32[]{:S(2)}) collective-permute-start(f32[3,2,32,260]{3,2,1,0:T(8,128)} %get-tuple-element.20), channel_id=1, source_target_pairs={{0,1},{1,2},{2,3},{3,4},{4,5},{5,6},{6,7},{8,9},{9,10},{10,11},{11... | collective-permute-start | bytes 599048 | tf_op jit(solution)/shard_map/ppermute | solution.py:21
  176.7 5.3 %copy-start.7 = (s32[64]{0:T(128)S(1)}, s32[64]{0:T(128)}, u32[]{:S(2)}) copy-start(s32[64]{0:T(128)} %copy-done.5) | copy-start | bytes 772
  176.7 17.9 %collective-permute-start.7 = (f32[3,2,32,260]{3,2,1,0:T(8,128)}, f32[3,2,32,260]{3,2,1,0:T(8,128)}, u32[]{:S(2)}, u32[]{:S(2)}) collective-permute-start(f32[3,2,32,260]{3,2,1,0:T(8,128)} %get-tuple-element.21), channel_id=1, source_target_pairs={{1,0},{2,1},{3,2},{4,3},{5,4},{6,5},{7,6},{9,8},{10,9},{11,10},{12... | collective-permute-start | bytes 599048 | tf_op jit(solution)/shard_map/ppermute | solution.py:22
  236.9 17.8 %copy-start.1 = (f32[3,16,32,256]{3,2,1,0:T(8,128)}, f32[3,16,32,256]{3,2,1,0:T(8,128)S(1)}, u32[]{:S(2)}) copy-start(f32[3,16,32,256]{3,2,1,0:T(8,128)S(1)} %divide_subtract_fusion) | copy-start | bytes 4718596
  237.6 7.5 %collective-permute-start.8 = (f32[3,16,32,1]{2,1,3,0:T(8,128)S(1)}, f32[3,16,32,1]{2,1,3,0:T(8,128)S(1)}, u32[]{:S(2)}, u32[]{:S(2)}) collective-permute-start(f32[3,16,32,1]{2,1,3,0:T(8,128)S(1)} %copy.129), channel_id=1, source_target_pairs={{0,8},{8,16},{16,24},{1,9},{9,17},{17,25},{2,10},{10,18},{18,26},{... | collective-permute-start | bytes 18440 | tf_op jit(solution)/shard_map/ppermute | solution.py:21
  241.8 5.1 %collective-permute-start.9 = (f32[3,16,32,1]{2,1,3,0:T(8,128)S(1)}, f32[3,16,32,1]{2,1,3,0:T(8,128)S(1)}, u32[]{:S(2)}, u32[]{:S(2)}) collective-permute-start(f32[3,16,32,1]{2,1,3,0:T(8,128)S(1)} %copy.130), channel_id=1, source_target_pairs={{8,0},{16,8},{24,16},{9,1},{17,9},{25,17},{10,2},{18,10},{26,18},{... | collective-permute-start | bytes 18440 | tf_op jit(solution)/shard_map/ppermute | solution.py:22
  247.5 3.4 %collective-permute-start.10 = (f32[3,1,32,258]{3,2,1,0:T(8,128)S(1)}, f32[3,1,32,258]{3,2,1,0:T(8,128)S(1)}, u32[]{:S(2)}, u32[]{:S(2)}) collective-permute-start(f32[3,1,32,258]{3,2,1,0:T(8,128)S(1)} %get-tuple-element.18), channel_id=1, source_target_pairs={{0,1},{1,2},{2,3},{3,4},{4,5},{5,6},{6,7},{8,9},{9,10},{10,11},{11... | collective-permute-start | bytes 297224 | tf_op jit(solution)/shard_map/ppermute | solution.py:21
  248.8 5.9 %collective-permute-start.11 = (f32[3,1,32,258]{3,2,1,0:T(8,128)S(1)}, f32[3,1,32,258]{3,2,1,0:T(8,128)S(1)}, u32[]{:S(2)}, u32[]{:S(2)}) collective-permute-start(f32[3,1,32,258]{3,2,1,0:T(8,128)S(1)} %get-tuple-element.19), channel_id=1, source_target_pairs={{1,0},{2,1},{3,2},{4,3},{5,4},{6,5},{7,6},{9,8},{10,9},{11,10},{12... | collective-permute-start | bytes 297224 | tf_op jit(solution)/shard_map/ppermute | solution.py:22
  258.1 1.7 copy-start.4
